TPU v7x, 128 devices: a whole 4x4x4 slice. The times are simulated.
128 devices in a mesh: pipe: 4 (over y_hi, core), exp: 16 (over x, z), pair: 2 (over y_lo).
Axes of the slice: x: 4, y: 4 (y_hi: 2, y_lo: 2; y = y_hi * 2 + y_lo), z: 4, core: 2. Of those that a mesh axis runs over, the one named last changes fastest.
Arguments:
- hidden_in: bfloat16 [4, 1024, 2048], P(None, ('exp', 'pair')), may hold values from -6 to 6
- routes: int32 [4, 4, 1024, 8], P('pipe', None, ('exp', 'pair')), may hold values from 0 to 63, all different within a row; in each aligned block of 32 rows (0 to 31, 32 to 63, ..., all dimensions but the last counted through in order) at most 6 rows name the same one
- gate_probs: float32 [4, 4, 1024, 8], P('pipe', None, ('exp', 'pair')), may hold values from 0.02 to 1
- norm_gain: float32 [4, 2048], P('pipe'), may hold values from 0.1 to 1.9
- w_gate: bfloat16 [4, 64, 2048, 768], P('pipe', ('exp', 'pair')), may hold values from -0.125 to 0.125
- w_up: bfloat16 [4, 64, 2048, 768], P('pipe', ('exp', 'pair')), may hold values from -0.125 to 0.125
- w_down: bfloat16 [4, 64, 768, 2048], P('pipe', ('exp', 'pair')), may hold values from -0.21875 to 0.21875
Outputs:
- layer_outputs: bfloat16 [4, 4, 1024, 2048], P('pipe', None, ('exp', 'pair'))
Inputs may be any that keep to these rules, and one draw needn't show every extreme that they name: `routes`: within each layer and micro-batch, the 32 tokens of one device (aligned blocks) name no expert more than 6 times in all, and each token names 8 different experts.
All inputs are finite; a program needn't handle non-finite values.
Results may differ from a plain program's by a relative error of at most 0.01.
Values may be sent and summed in bfloat16 or wider, within the bound.
A program may use at most 64 MiB of HBM per device.

v0:
```python
import jax
import jax.numpy as jnp
from jax import lax
from jax.sharding import PartitionSpec as P

EPS = 1e-06


def passed_along(value, axis, steps):
    count = lax.axis_size(axis)
    first, last = (max(0, -steps), min(count, count - steps))
    return lax.ppermute(value, axis, [(source, source + steps) for source in range(first, last)])


def expert_block(arrived, wgate, wupper, wdown):
    gate = jnp.einsum("nlcd,ldf->nlcf", arrived, wgate, preferred_element_type=jnp.float32)
    upward = jnp.einsum("nlcd,ldf->nlcf", arrived, wupper, preferred_element_type=jnp.float32)
    hidden = (jax.nn.silu(gate) * upward).astype(jnp.bfloat16)
    return jnp.einsum("nlcf,lfd->nlcd", hidden, wdown, preferred_element_type=jnp.float32).astype(
        jnp.bfloat16
    )


def on_device(hidden_in, routes, gate_probs, norm_gain, w_gate, w_up, w_down):
    section = lax.axis_index("pipe")
    micro, tok_rows, width = hidden_in.shape
    top_count = routes.shape[3]
    groups = lax.axis_size(("exp", "pair"))
    local_experts = w_gate.shape[1]
    experts = local_experts * groups
    capacity = max(2, 3 * tok_rows * top_count // (2 * experts))
    gain = norm_gain[0]
    wgate = w_gate[0]
    wupper = w_up[0]
    wdown = w_down[0]
    expert_ids = jnp.arange(experts, dtype=jnp.int32)

    def layer(state, index):
        chosen = lax.dynamic_index_in_dim(routes[0], index, 0, keepdims=False).reshape(-1)
        probs = lax.dynamic_index_in_dim(gate_probs[0], index, 0, keepdims=False)
        floated = state.astype(jnp.float32)
        scale = lax.rsqrt(jnp.mean(floated * floated, axis=-1, keepdims=True) + EPS)
        normed = (floated * scale * gain).astype(jnp.bfloat16)
        onehot = (chosen[:, None] == expert_ids[None, :]).astype(jnp.int32)
        before = jnp.cumsum(onehot, axis=0) - onehot
        slots = jnp.sum(before * onehot, axis=1)
        outgoing = jnp.zeros((experts, capacity, width), jnp.bfloat16)
        outgoing = outgoing.at[chosen, slots].set(jnp.repeat(normed, top_count, axis=0))
        grouped = outgoing.reshape(groups, local_experts, capacity, width)
        produced = expert_block(
            lax.all_to_all(grouped, ("exp", "pair"), split_axis=0, concat_axis=0, tiled=True),
            wgate,
            wupper,
            wdown,
        )
        returned = lax.all_to_all(
            produced, ("exp", "pair"), split_axis=0, concat_axis=0, tiled=True
        )
        results = returned.reshape(experts, capacity, width)[chosen, slots]
        results = results.reshape(tok_rows, top_count, width).astype(jnp.float32)
        weights = probs / jnp.sum(probs, axis=-1, keepdims=True)
        mixed = jnp.einsum("tk,tkd->td", weights, results)
        return (floated + mixed).astype(jnp.bfloat16)

    def advance(step, carry):
        received, saved = carry
        index = step - section
        valid = jnp.logical_and(index >= 0, index < micro)
        clipped = jnp.clip(index, 0, micro - 1)
        first = lax.dynamic_index_in_dim(hidden_in, clipped, 0, keepdims=False)
        state = jnp.where(section == 0, first, received)
        updated = layer(state, clipped)
        saved = jnp.where(valid, lax.dynamic_update_index_in_dim(saved, updated, clipped, 0), saved)
        received = passed_along(updated, "pipe", 1)
        return (received, saved)

    start = (
        jnp.zeros((tok_rows, width), jnp.bfloat16),
        jnp.zeros((micro, tok_rows, width), jnp.bfloat16),
    )
    received, saved = lax.fori_loop(0, micro + lax.axis_size("pipe") - 1, advance, start)
    return saved[None]


def solution(mesh):
    in_specs = (
        P(None, ("exp", "pair"), None),
        P("pipe", None, ("exp", "pair"), None),
        P("pipe", None, ("exp", "pair"), None),
        P("pipe", None),
        P("pipe", ("exp", "pair"), None, None),
        P("pipe", ("exp", "pair"), None, None),
        P("pipe", ("exp", "pair"), None, None),
    )
    out_specs = P("pipe", None, ("exp", "pair"), None)
    return jax.shard_map(
        on_device, mesh=mesh, in_specs=in_specs, out_specs=out_specs, check_vma=False
    )
```

profile of v0, /device:TPU:1, one launch (start us, length us, event | category | flops | bytes accessed | tf_op | source)
XLA Modules:
  0.0 810.6 jit_solution(4806493436090635416)
XLA Ops:
  0.9 809.7 %while.18 = (s32[]{:T(128)}, bf16[32,2048]{1,0:T(8,128)(2,1)S(1)}, bf16[4,32,2048]{2,1,0:T(8,128)(2,1)}, pred[]{:T(512)}, s32[]{:T(128)}, /*index=5*/bf16[4,32,2...) while((s32[]{:T(128)}, bf16[32,2048]{1,0:T(8,128)(2,1)S(1)}, ...), condition=%wide.region_7.8_spmd.clone.clone, body=%wide.region_0.7_spmd.clone.clone.sunk | while | flops 3630486016 | bytes 61134680 | solution.py:81
  5.1 22.3 %scatter_fusion = bf16[64,6,2048]{2,0,1:T(8,128)(2,1)S(1)} fusion(bf16[64,6,2048]{2,0,1:T(8,128)(2,1)S(1)} %broadcast.267, s32[256]{0:T(256)S(1)} %bitcast.139, bf16[256,2048]{1,0:T(8,128)(2,1)S(1)} %broadcast_bitcast_fusion.2), kind=kCustom, calls=%fused_computation.1.clone.clone.1 | custom fusion | bytes 3147776 | tf_op jit(solution)/shard_map/while/body/eval_jaxpr/scatter | solution.py:48
  30.2 31.6 %all_to_all.26 = bf16[32,2,6,2048]{3,1,2,0:T(2,128)(2,1)S(1)} all-to-all(bf16[32,2,6,2048]{3,1,2,0:T(2,128)(2,1)S(1)} %copy.58), channel_id=1, replica_groups=mesh['pipe'=4,'exp'=16,'pair'=2] {'exp','pair'}, dimensions={0} | all-to-all | bytes 3145728 | tf_op jit(solution)/shard_map/while/body/eval_jaxpr/all_to_all | solution.py:51
  61.8 6.4 fusion.86
  68.2 8.9 %fusion.87 = bf16[32,2,6,2048]{3,0,2,1:T(8,128)(2,1)S(1)} fusion(bf16[2,768,2048]{2,1,0:T(8,128)(2,1)} %get-tuple-element.525, bf16[2,2048,768]{2,1,0:T(8,128)(2,1)} %get-tuple-element.524, bf16[32,2,6,2048]{3,1,2,0:T(2,128)(2,1)S(1)} %all_to_all.26, f32[32,2,6,768]{3,0,2,1:T(8,128)} %fusion.86), kind=kOutput, calls=%fused_computation.10.clone.1 | convolution fusion | flops 2418475008 | bytes 16908288 | tf_op jit(solution)/shard_map/while/body/eval_jaxpr/nlcf,lfd->nlcd/dot_general | solution.py:19
  84.6 20.8 %all-to-all-done.1 = bf16[32,2,6,2048]{3,1,2,0:T(2,128)(2,1)S(1)} async-done(((bf16[32,2,6,2048]{3,1,2,0:T(2,128)(2,1)}), bf16[32,2,6,2048]{3,1,2,0:T(2,128)(2,1)S(1)}, u32[]{:S(2)}, u32[]{:S(2)}) %all-to-all-start.1) | async-done | bytes 1572896 | tf_op jit(solution)/shard_map/while/body/eval_jaxpr/all_to_all | solution.py:56
  113.6 7.4 collective-permute-start
  127.1 22.3 %scatter_fusion = bf16[64,6,2048]{2,0,1:T(8,128)(2,1)S(1)} fusion(bf16[64,6,2048]{2,0,1:T(8,128)(2,1)S(1)} %broadcast.267, s32[256]{0:T(256)S(1)} %bitcast.139, bf16[256,2048]{1,0:T(8,128)(2,1)S(1)} %broadcast_bitcast_fusion.2), kind=kCustom, calls=%fused_computation.1.clone.clone.1 | custom fusion | bytes 3147776 | tf_op jit(solution)/shard_map/while/body/eval_jaxpr/scatter | solution.py:48
  152.1 24.9 %all_to_all.26 = bf16[32,2,6,2048]{3,1,2,0:T(2,128)(2,1)S(1)} all-to-all(bf16[32,2,6,2048]{3,1,2,0:T(2,128)(2,1)S(1)} %copy.58), channel_id=1, replica_groups=mesh['pipe'=4,'exp'=16,'pair'=2] {'exp','pair'}, dimensions={0} | all-to-all | bytes 3145728 | tf_op jit(solution)/shard_map/while/body/eval_jaxpr/all_to_all | solution.py:51
  177.1 6.4 fusion.86
  183.5 8.9 %fusion.87 = bf16[32,2,6,2048]{3,0,2,1:T(8,128)(2,1)S(1)} fusion(bf16[2,768,2048]{2,1,0:T(8,128)(2,1)} %get-tuple-element.525, bf16[2,2048,768]{2,1,0:T(8,128)(2,1)} %get-tuple-element.524, bf16[32,2,6,2048]{3,1,2,0:T(2,128)(2,1)S(1)} %all_to_all.26, f32[32,2,6,768]{3,0,2,1:T(8,128)} %fusion.86), kind=kOutput, calls=%fused_computation.10.clone.1 | convolution fusion | flops 2418475008 | bytes 16908288 | tf_op jit(solution)/shard_map/while/body/eval_jaxpr/nlcf,lfd->nlcd/dot_general | solution.py:19
  199.4 22.3 %all-to-all-done.1 = bf16[32,2,6,2048]{3,1,2,0:T(2,128)(2,1)S(1)} async-done(((bf16[32,2,6,2048]{3,1,2,0:T(2,128)(2,1)}), bf16[32,2,6,2048]{3,1,2,0:T(2,128)(2,1)S(1)}, u32[]{:S(2)}, u32[]{:S(2)}) %all-to-all-start.1) | async-done | bytes 1572896 | tf_op jit(solution)/shard_map/while/body/eval_jaxpr/all_to_all | solution.py:56
  238.0 22.3 %scatter_fusion = bf16[64,6,2048]{2,0,1:T(8,128)(2,1)S(1)} fusion(bf16[64,6,2048]{2,0,1:T(8,128)(2,1)S(1)} %broadcast.267, s32[256]{0:T(256)S(1)} %bitcast.139, bf16[256,2048]{1,0:T(8,128)(2,1)S(1)} %broadcast_bitcast_fusion.2), kind=kCustom, calls=%fused_computation.1.clone.clone.1 | custom fusion | bytes 3147776 | tf_op jit(solution)/shard_map/while/body/eval_jaxpr/scatter | solution.py:48
  263.0 28.1 %all_to_all.26 = bf16[32,2,6,2048]{3,1,2,0:T(2,128)(2,1)S(1)} all-to-all(bf16[32,2,6,2048]{3,1,2,0:T(2,128)(2,1)S(1)} %copy.58), channel_id=1, replica_groups=mesh['pipe'=4,'exp'=16,'pair'=2] {'exp','pair'}, dimensions={0} | all-to-all | bytes 3145728 | tf_op jit(solution)/shard_map/while/body/eval_jaxpr/all_to_all | solution.py:51
  297.6 8.9 %fusion.87 = bf16[32,2,6,2048]{3,0,2,1:T(8,128)(2,1)S(1)} fusion(bf16[2,768,2048]{2,1,0:T(8,128)(2,1)} %get-tuple-element.525, bf16[2,2048,768]{2,1,0:T(8,128)(2,1)} %get-tuple-element.524, bf16[32,2,6,2048]{3,1,2,0:T(2,128)(2,1)S(1)} %all_to_all.26, f32[32,2,6,768]{3,0,2,1:T(8,128)} %fusion.86), kind=kOutput, calls=%fused_computation.10.clone.1 | convolution fusion | flops 2418475008 | bytes 16908288 | tf_op jit(solution)/shard_map/while/body/eval_jaxpr/nlcf,lfd->nlcd/dot_general | solution.py:19
  314.2 22.2 %all-to-all-done.1 = bf16[32,2,6,2048]{3,1,2,0:T(2,128)(2,1)S(1)} async-done(((bf16[32,2,6,2048]{3,1,2,0:T(2,128)(2,1)}), bf16[32,2,6,2048]{3,1,2,0:T(2,128)(2,1)S(1)}, u32[]{:S(2)}, u32[]{:S(2)}) %all-to-all-start.1) | async-done | bytes 1572896 | tf_op jit(solution)/shard_map/while/body/eval_jaxpr/all_to_all | solution.py:56
  352.8 22.3 %scatter_fusion = bf16[64,6,2048]{2,0,1:T(8,128)(2,1)S(1)} fusion(bf16[64,6,2048]{2,0,1:T(8,128)(2,1)S(1)} %broadcast.267, s32[256]{0:T(256)S(1)} %bitcast.139, bf16[256,2048]{1,0:T(8,128)(2,1)S(1)} %broadcast_bitcast_fusion.2), kind=kCustom, calls=%fused_computation.1.clone.clone.1 | custom fusion | bytes 3147776 | tf_op jit(solution)/shard_map/while/body/eval_jaxpr/scatter | solution.py:48
  377.8 29.0 %all_to_all.26 = bf16[32,2,6,2048]{3,1,2,0:T(2,128)(2,1)S(1)} all-to-all(bf16[32,2,6,2048]{3,1,2,0:T(2,128)(2,1)S(1)} %copy.58), channel_id=1, replica_groups=mesh['pipe'=4,'exp'=16,'pair'=2] {'exp','pair'}, dimensions={0} | all-to-all | bytes 3145728 | tf_op jit(solution)/shard_map/while/body/eval_jaxpr/all_to_all | solution.py:51
  413.2 8.9 %fusion.87 = bf16[32,2,6,2048]{3,0,2,1:T(8,128)(2,1)S(1)} fusion(bf16[2,768,2048]{2,1,0:T(8,128)(2,1)} %get-tuple-element.525, bf16[2,2048,768]{2,1,0:T(8,128)(2,1)} %get-tuple-element.524, bf16[32,2,6,2048]{3,1,2,0:T(2,128)(2,1)S(1)} %all_to_all.26, f32[32,2,6,768]{3,0,2,1:T(8,128)} %fusion.86), kind=kOutput, calls=%fused_computation.10.clone.1 | convolution fusion | flops 2418475008 | bytes 16908288 | tf_op jit(solution)/shard_map/while/body/eval_jaxpr/nlcf,lfd->nlcd/dot_general | solution.py:19
  429.8 22.2 %all-to-all-done.1 = bf16[32,2,6,2048]{3,1,2,0:T(2,128)(2,1)S(1)} async-done(((bf16[32,2,6,2048]{3,1,2,0:T(2,128)(2,1)}), bf16[32,2,6,2048]{3,1,2,0:T(2,128)(2,1)S(1)}, u32[]{:S(2)}, u32[]{:S(2)}) %all-to-all-start.1) | async-done | bytes 1572896 | tf_op jit(solution)/shard_map/while/body/eval_jaxpr/all_to_all | solution.py:56
  468.4 22.3 %scatter_fusion = bf16[64,6,2048]{2,0,1:T(8,128)(2,1)S(1)} fusion(bf16[64,6,2048]{2,0,1:T(8,128)(2,1)S(1)} %broadcast.267, s32[256]{0:T(256)S(1)} %bitcast.139, bf16[256,2048]{1,0:T(8,128)(2,1)S(1)} %broadcast_bitcast_fusion.2), kind=kCustom, calls=%fused_computation.1.clone.clone.1 | custom fusion | bytes 3147776 | tf_op jit(solution)/shard_map/while/body/eval_jaxpr/scatter | solution.py:48
  493.4 28.9 %all_to_all.26 = bf16[32,2,6,2048]{3,1,2,0:T(2,128)(2,1)S(1)} all-to-all(bf16[32,2,6,2048]{3,1,2,0:T(2,128)(2,1)S(1)} %copy.58), channel_id=1, replica_groups=mesh['pipe'=4,'exp'=16,'pair'=2] {'exp','pair'}, dimensions={0} | all-to-all | bytes 3145728 | tf_op jit(solution)/shard_map/while/body/eval_jaxpr/all_to_all | solution.py:51
  528.7 8.9 %fusion.87 = bf16[32,2,6,2048]{3,0,2,1:T(8,128)(2,1)S(1)} fusion(bf16[2,768,2048]{2,1,0:T(8,128)(2,1)} %get-tuple-element.525, bf16[2,2048,768]{2,1,0:T(8,128)(2,1)} %get-tuple-element.524, bf16[32,2,6,2048]{3,1,2,0:T(2,128)(2,1)S(1)} %all_to_all.26, f32[32,2,6,768]{3,0,2,1:T(8,128)} %fusion.86), kind=kOutput, calls=%fused_computation.10.clone.1 | convolution fusion | flops 2418475008 | bytes 16908288 | tf_op jit(solution)/shard_map/while/body/eval_jaxpr/nlcf,lfd->nlcd/dot_general | solution.py:19
  545.3 22.2 %all-to-all-done.1 = bf16[32,2,6,2048]{3,1,2,0:T(2,128)(2,1)S(1)} async-done(((bf16[32,2,6,2048]{3,1,2,0:T(2,128)(2,1)}), bf16[32,2,6,2048]{3,1,2,0:T(2,128)(2,1)S(1)}, u32[]{:S(2)}, u32[]{:S(2)}) %all-to-all-start.1) | async-done | bytes 1572896 | tf_op jit(solution)/shard_map/while/body/eval_jaxpr/all_to_all | solution.py:56
  583.9 22.3 %scatter_fusion = bf16[64,6,2048]{2,0,1:T(8,128)(2,1)S(1)} fusion(bf16[64,6,2048]{2,0,1:T(8,128)(2,1)S(1)} %broadcast.267, s32[256]{0:T(256)S(1)} %bitcast.139, bf16[256,2048]{1,0:T(8,128)(2,1)S(1)} %broadcast_bitcast_fusion.2), kind=kCustom, calls=%fused_computation.1.clone.clone.1 | custom fusion | bytes 3147776 | tf_op jit(solution)/shard_map/while/body/eval_jaxpr/scatter | solution.py:48
  608.9 28.9 %all_to_all.26 = bf16[32,2,6,2048]{3,1,2,0:T(2,128)(2,1)S(1)} all-to-all(bf16[32,2,6,2048]{3,1,2,0:T(2,128)(2,1)S(1)} %copy.58), channel_id=1, replica_groups=mesh['pipe'=4,'exp'=16,'pair'=2] {'exp','pair'}, dimensions={0} | all-to-all | bytes 3145728 | tf_op jit(solution)/shard_map/while/body/eval_jaxpr/all_to_all | solution.py:51
  644.2 8.9 %fusion.87 = bf16[32,2,6,2048]{3,0,2,1:T(8,128)(2,1)S(1)} fusion(bf16[2,768,2048]{2,1,0:T(8,128)(2,1)} %get-tuple-element.525, bf16[2,2048,768]{2,1,0:T(8,128)(2,1)} %get-tuple-element.524, bf16[32,2,6,2048]{3,1,2,0:T(2,128)(2,1)S(1)} %all_to_all.26, f32[32,2,6,768]{3,0,2,1:T(8,128)} %fusion.86), kind=kOutput, calls=%fused_computation.10.clone.1 | convolution fusion | flops 2418475008 | bytes 16908288 | tf_op jit(solution)/shard_map/while/body/eval_jaxpr/nlcf,lfd->nlcd/dot_general | solution.py:19
  660.8 22.2 %all-to-all-done.1 = bf16[32,2,6,2048]{3,1,2,0:T(2,128)(2,1)S(1)} async-done(((bf16[32,2,6,2048]{3,1,2,0:T(2,128)(2,1)}), bf16[32,2,6,2048]{3,1,2,0:T(2,128)(2,1)S(1)}, u32[]{:S(2)}, u32[]{:S(2)}) %all-to-all-start.1) | async-done | bytes 1572896 | tf_op jit(solution)/shard_map/while/body/eval_jaxpr/all_to_all | solution.py:56
  699.4 22.3 %scatter_fusion = bf16[64,6,2048]{2,0,1:T(8,128)(2,1)S(1)} fusion(bf16[64,6,2048]{2,0,1:T(8,128)(2,1)S(1)} %broadcast.267, s32[256]{0:T(256)S(1)} %bitcast.139, bf16[256,2048]{1,0:T(8,128)(2,1)S(1)} %broadcast_bitcast_fusion.2), kind=kCustom, calls=%fused_computation.1.clone.clone.1 | custom fusion | bytes 3147776 | tf_op jit(solution)/shard_map/while/body/eval_jaxpr/scatter | solution.py:48
  724.4 28.9 %all_to_all.26 = bf16[32,2,6,2048]{3,1,2,0:T(2,128)(2,1)S(1)} all-to-all(bf16[32,2,6,2048]{3,1,2,0:T(2,128)(2,1)S(1)} %copy.58), channel_id=1, replica_groups=mesh['pipe'=4,'exp'=16,'pair'=2] {'exp','pair'}, dimensions={0} | all-to-all | bytes 3145728 | tf_op jit(solution)/shard_map/while/body/eval_jaxpr/all_to_all | solution.py:51
  759.7 8.9 %fusion.87 = bf16[32,2,6,2048]{3,0,2,1:T(8,128)(2,1)S(1)} fusion(bf16[2,768,2048]{2,1,0:T(8,128)(2,1)} %get-tuple-element.525, bf16[2,2048,768]{2,1,0:T(8,128)(2,1)} %get-tuple-element.524, bf16[32,2,6,2048]{3,1,2,0:T(2,128)(2,1)S(1)} %all_to_all.26, f32[32,2,6,768]{3,0,2,1:T(8,128)} %fusion.86), kind=kOutput, calls=%fused_computation.10.clone.1 | convolution fusion | flops 2418475008 | bytes 16908288 | tf_op jit(solution)/shard_map/while/body/eval_jaxpr/nlcf,lfd->nlcd/dot_general | solution.py:19
  776.3 22.2 %all-to-all-done.1 = bf16[32,2,6,2048]{3,1,2,0:T(2,128)(2,1)S(1)} async-done(((bf16[32,2,6,2048]{3,1,2,0:T(2,128)(2,1)}), bf16[32,2,6,2048]{3,1,2,0:T(2,128)(2,1)S(1)}, u32[]{:S(2)}, u32[]{:S(2)}) %all-to-all-start.1) | async-done | bytes 1572896 | tf_op jit(solution)/shard_map/while/body/eval_jaxpr/all_to_all | solution.py:56
  (237 shorter events, 216.3 us)
Async XLA Ops:
  79.9 4.5 copy-start
  79.9 25.4 %all-to-all-start.1 = ((bf16[32,2,6,2048]{3,1,2,0:T(2,128)(2,1)}), bf16[32,2,6,2048]{3,1,2,0:T(2,128)(2,1)S(1)}, u32[]{:S(2)}, u32[]{:S(2)}) async-start(bf16[32,2,6,2048]{3,1,2,0:T(2,128)(2,1)} %copy.59), calls=%async_computation.1 | async-start | bytes 3145728 | tf_op jit(solution)/shard_map/while/body/eval_jaxpr/all_to_all | solution.py:56
  113.6 9.3 %collective-permute-start = (bf16[32,2048]{1,0:T(8,128)(2,1)S(1)}, bf16[32,2048]{1,0:T(8,128)(2,1)S(1)}, u32[]{:S(2)}, u32[]{:S(2)}) collective-permute-start(bf16[32,2048]{1,0:T(8,128)(2,1)S(1)} %get-tuple-element.478), channel_id=1, source_target_pairs={{0,32},{32,64},{64,96},{1,33},{33,65},{65,97},{2,34},{34,66},{66,9... | collective-permute-start | bytes 393224 | tf_op jit(solution)/shard_map/while/body/eval_jaxpr/ppermute | solution.py:12
  195.2 4.1 copy-start
  195.2 26.5 %all-to-all-start.1 = ((bf16[32,2,6,2048]{3,1,2,0:T(2,128)(2,1)}), bf16[32,2,6,2048]{3,1,2,0:T(2,128)(2,1)S(1)}, u32[]{:S(2)}, u32[]{:S(2)}) async-start(bf16[32,2,6,2048]{3,1,2,0:T(2,128)(2,1)} %copy.59), calls=%async_computation.1 | async-start | bytes 3145728 | tf_op jit(solution)/shard_map/while/body/eval_jaxpr/all_to_all | solution.py:56
  229.9 3.8 collective-permute-start
  309.3 4.8 copy-start
  309.3 27.2 %all-to-all-start.1 = ((bf16[32,2,6,2048]{3,1,2,0:T(2,128)(2,1)}), bf16[32,2,6,2048]{3,1,2,0:T(2,128)(2,1)S(1)}, u32[]{:S(2)}, u32[]{:S(2)}) async-start(bf16[32,2,6,2048]{3,1,2,0:T(2,128)(2,1)} %copy.59), calls=%async_computation.1 | async-start | bytes 3145728 | tf_op jit(solution)/shard_map/while/body/eval_jaxpr/all_to_all | solution.py:56
  344.7 3.8 collective-permute-start
  424.9 4.8 copy-start
  424.9 27.2 %all-to-all-start.1 = ((bf16[32,2,6,2048]{3,1,2,0:T(2,128)(2,1)}), bf16[32,2,6,2048]{3,1,2,0:T(2,128)(2,1)S(1)}, u32[]{:S(2)}, u32[]{:S(2)}) async-start(bf16[32,2,6,2048]{3,1,2,0:T(2,128)(2,1)} %copy.59), calls=%async_computation.1 | async-start | bytes 3145728 | tf_op jit(solution)/shard_map/while/body/eval_jaxpr/all_to_all | solution.py:56
  460.3 3.8 collective-permute-start
  540.4 4.8 copy-start
  540.4 27.2 %all-to-all-start.1 = ((bf16[32,2,6,2048]{3,1,2,0:T(2,128)(2,1)}), bf16[32,2,6,2048]{3,1,2,0:T(2,128)(2,1)S(1)}, u32[]{:S(2)}, u32[]{:S(2)}) async-start(bf16[32,2,6,2048]{3,1,2,0:T(2,128)(2,1)} %copy.59), calls=%async_computation.1 | async-start | bytes 3145728 | tf_op jit(solution)/shard_map/while/body/eval_jaxpr/all_to_all | solution.py:56
  575.8 3.8 collective-permute-start
  655.9 4.8 copy-start
  655.9 27.2 %all-to-all-start.1 = ((bf16[32,2,6,2048]{3,1,2,0:T(2,128)(2,1)}), bf16[32,2,6,2048]{3,1,2,0:T(2,128)(2,1)S(1)}, u32[]{:S(2)}, u32[]{:S(2)}) async-start(bf16[32,2,6,2048]{3,1,2,0:T(2,128)(2,1)} %copy.59), calls=%async_computation.1 | async-start | bytes 3145728 | tf_op jit(solution)/shard_map/while/body/eval_jaxpr/all_to_all | solution.py:56
  691.3 3.8 collective-permute-start
  771.4 4.8 copy-start
  771.4 27.2 %all-to-all-start.1 = ((bf16[32,2,6,2048]{3,1,2,0:T(2,128)(2,1)}), bf16[32,2,6,2048]{3,1,2,0:T(2,128)(2,1)S(1)}, u32[]{:S(2)}, u32[]{:S(2)}) async-start(bf16[32,2,6,2048]{3,1,2,0:T(2,128)(2,1)} %copy.59), calls=%async_computation.1 | async-start | bytes 3145728 | tf_op jit(solution)/shard_map/while/body/eval_jaxpr/all_to_all | solution.py:56
  806.8 3.8 collective-permute-start
where the time goes:
time: 813 us; the launch traced here: 811 us
  local copies, waits for them, and re-layouts  250 us (31%)
  blocking collectives  200 us (25%)
  waiting for transfers between devices  168 us (21%)
  matrix products  110 us (14%)
  starting transfers between devices  51.2 us (6%)
  other arithmetic  30.6 us (4%)
    all_to_all x7, blocking collectives, layer(): lax.all_to_all(grouped, ('exp', 'pair'), split_axis=0, concat_axis=0, til...  200 us
    scatter x7, local copies, waits for them, and re-layouts, layer(): outgoing.at[chosen, slots].set(jnp.repeat(normed, top_count, axis=0))  156 us
    all_to_all x7, waiting for transfers between devices, layer(): lax.all_to_all(produced, ('exp', 'pair'), split_axis=0, concat_axis=0, ti...  154 us
    dot_general x7, matrix products, expert_block(): jnp.einsum('nlcf,lfd->nlcd', hidden, wdown, preferred_element_type=jnp.fl...  62.2 us
    dot_general x7, matrix products, expert_block(): jnp.einsum('nlcd,ldf->nlcf', arrived, wgate, preferred_element_type=jnp.f...  45 us
    all_to_all x7, starting transfers between devices, layer(): lax.all_to_all(produced, ('exp', 'pair'), split_axis=0, concat_axis=0, ti...  32.4 us
    gather x7, local copies, waits for them, and re-layouts, layer(): results = returned.reshape(experts, capacity, width)[chosen, slots]  30.1 us
    convert_element_type x7, local copies, waits for them, and re-layouts, expert_block(): jnp.einsum('nlcf,lfd->nlcd', hidden, wdown, preferred_element_type=jnp.fl...  19.5 us
  transfers between devices with their start and end apart: 14, of which 14 were waited for; matrix products, arithmetic and copies ran while one was open for 0% of the time, Pallas kernels for 0%

commit v1 on v0

v1 whole, which is shorter than its diff:
```python
import functools

import jax
import jax.numpy as jnp
from jax import lax
from jax.experimental import pallas as pl
from jax.experimental.pallas import tpu as pltpu
from jax.sharding import PartitionSpec as P

EPS = 1e-06
MESH = pl.DeviceIdType.MESH
BF16 = jnp.bfloat16
F32 = jnp.float32
SIDE = 4
COLS = 256


def kernel(stages, groups, cap, hidden_ref, routes_ref, probs_ref, gain_ref, wg_hbm, wu_hbm, wd_hbm, out_ref,
           wg, wu, wd, send, recv, back, done, relay, state, normed, rows, hid, total, pick, mix,
           w_sem, d_send, d_recv, r_send, r_recv, n_send, n_recv):
    stage, exp, pair = lax.axis_index("pipe"), lax.axis_index("exp"), lax.axis_index("pair")
    pairs = lax.axis_size("pair")
    me = exp * pairs + pair
    micro, tok, width = hidden_ref.shape
    top = routes_ref.shape[2]
    local, _, slots, _ = send.shape[1:]
    span = groups * slots
    hidden_units = wg.shape[2]

    def weight_copies(e):
        return [pltpu.make_async_copy(hbm.at[e], vmem.at[e], w_sem.at[i, e])
                for i, (hbm, vmem) in enumerate(((wg_hbm, wg), (wu_hbm, wu), (wd_hbm, wd)))]

    for e in range(local):
        for copy in weight_copies(e):
            copy.start()

    barrier = pltpu.get_barrier_semaphore()

    def greet(i, carry):
        peer = lax.rem(me + i, groups)
        pl.semaphore_signal(barrier, inc=1, device_id=(stage, peer // pairs, lax.rem(peer, pairs)), device_id_type=MESH)
        return carry

    lax.fori_loop(1, groups, greet, 0)

    @pl.when(stage > 0)
    def _():
        pl.semaphore_signal(barrier, inc=1, device_id=(stage - 1, exp, pair), device_id_type=MESH)

    def prepare(m):
        column = lax.broadcasted_iota(jnp.int32, (tok, local * groups), 1)
        expert = lax.rem(column, groups) * local + column // groups
        probs = probs_ref[m]
        probs = probs / jnp.sum(probs, axis=-1, keepdims=True)
        routes = routes_ref[m]
        named = jnp.zeros((tok, local * groups), F32)
        weight = jnp.zeros((tok, local * groups), F32)
        for k in range(top):
            hit = routes[:, k:k + 1] == expert
            named = named + jnp.where(hit, 1.0, 0.0)
            weight = weight + jnp.where(hit, probs[:, k:k + 1], 0.0)
        earlier = lax.broadcasted_iota(jnp.int32, (tok, tok), 1) < lax.broadcasted_iota(jnp.int32, (tok, tok), 0)
        before = jnp.dot(jnp.where(earlier, 1.0, 0.0).astype(BF16), named.astype(BF16), preferred_element_type=F32)
        high = weight.astype(BF16)
        low = (weight - high.astype(F32)).astype(BF16)
        shape = (local * groups, local * span)
        spread = jnp.where(lax.broadcasted_iota(jnp.int32, shape, 1) // slots == lax.broadcasted_iota(jnp.int32, shape, 0), 1.0, 0.0)
        spread = spread.astype(BF16)
        slot = lax.rem(lax.broadcasted_iota(jnp.int32, (tok, local * span), 1), slots).astype(F32)
        taken = jnp.dot(named.astype(BF16), spread, preferred_element_type=F32)
        place = jnp.dot(before.astype(BF16), spread, preferred_element_type=F32)
        mask = jnp.logical_and(taken > 0.5, jnp.abs(place - slot) < 0.5)
        mix[m, 0:tok, :] = jnp.where(mask, jnp.dot(high, spread, preferred_element_type=F32), 0.0).astype(BF16)
        mix[m, tok:2 * tok, :] = jnp.where(mask, jnp.dot(low, spread, preferred_element_type=F32), 0.0).astype(BF16)
        pick[m] = jnp.where(mask, 1.0, 0.0).T.astype(BF16)

    prepare(0)
    pl.semaphore_wait(barrier, groups - 1 + jnp.minimum(stages - 1 - stage, 1))

    offsets = [(dx, dz, dy) for dx in range(SIDE) for dz in range(SIDE) for dy in range(2)][1:]

    def exchange(source, target, m, e, s_sem, r_sem):
        x, z = exp // SIDE, lax.rem(exp, SIDE)
        for dx, dz, dy in offsets:
            peer_exp = lax.rem(x + dx, SIDE) * SIDE + lax.rem(z + dz, SIDE)
            peer_pair = lax.rem(pair + dy, pairs)
            peer = peer_exp * pairs + peer_pair
            pltpu.make_async_remote_copy(
                src_ref=source.at[m, e, peer, pl.ds(0, cap)],
                dst_ref=target.at[m, e, me, pl.ds(0, cap)],
                send_sem=s_sem.at[m, e],
                recv_sem=r_sem.at[m, e],
                device_id=(stage, peer_exp, peer_pair),
                device_id_type=MESH,
            ).start()
        target[m, e, me] = source[m, e, me]

    def arrived(buffer, m, e, sem):
        part = buffer.at[m, e, pl.ds(0, groups - 1), pl.ds(0, cap)]
        pltpu.make_async_copy(part, part, sem.at[m, e]).wait()

    def relay_copy(m, target_stage):
        return pltpu.make_async_remote_copy(
            src_ref=out_ref.at[m], dst_ref=relay.at[m], send_sem=n_send.at[m], recv_sem=n_recv.at[m],
            device_id=(target_stage, exp, pair), device_id_type=MESH)

    def one(m, carry):
        @pl.when(stage == 0)
        def _():
            state[...] = hidden_ref[m].astype(F32)

        @pl.when(stage > 0)
        def _():
            relay_copy(m, stage).wait_recv()
            state[...] = relay[m].astype(F32)

        floated = state[...]
        scale = lax.rsqrt(jnp.mean(floated * floated, axis=-1, keepdims=True) + EPS)
        normed[...] = (floated * scale * gain_ref[...]).astype(BF16)

        def dispatch(e, carry):
            begin = pl.multiple_of(e * span, span)
            for c in range(0, width, COLS):
                made = jnp.dot(pick[m, pl.ds(begin, span), :], normed[:, c:c + COLS], preferred_element_type=F32)
                send[m, e, :, :, c:c + COLS] = made.reshape(groups, slots, COLS).astype(BF16)
            exchange(send, recv, m, e, d_send, d_recv)
            return carry

        lax.fori_loop(0, local, dispatch, 0)
        done[m, :, :, cap:slots, :] = jnp.zeros((local, groups, slots - cap, width), BF16)

        def ffn(e, carry):
            @pl.when(m == 0)
            def _():
                for copy in weight_copies(e):
                    copy.wait()

            arrived(recv, m, e, d_recv)
            rows[...] = recv[m, e].reshape(span, width)
            for c in range(0, hidden_units, COLS):
                gate = jnp.dot(rows[...], wg[e, :, c:c + COLS], preferred_element_type=F32)
                upward = jnp.dot(rows[...], wu[e, :, c:c + COLS], preferred_element_type=F32)
                hid[:, c:c + COLS] = (jax.nn.silu(gate) * upward).astype(BF16)
            for c in range(0, width, COLS):
                made = jnp.dot(hid[...], wd[e, :, c:c + COLS], preferred_element_type=F32)
                back[m, e, :, :, c:c + COLS] = made.reshape(groups, slots, COLS).astype(BF16)
            exchange(back, done, m, e, r_send, r_recv)
            return carry

        lax.fori_loop(0, local, ffn, 0)

        @pl.when(m + 1 < micro)
        def _():
            prepare(m + 1)

        total[...] = jnp.zeros_like(total)

        def combine(e, carry):
            arrived(done, m, e, r_recv)
            begin = pl.multiple_of(e * span, span)
            for c in range(0, width, COLS):
                total[:, c:c + COLS] += jnp.dot(mix[m, :, pl.ds(begin, span)],
                                                done[m, e, :, :, c:c + COLS].reshape(span, COLS), preferred_element_type=F32)
            return carry

        lax.fori_loop(0, local, combine, 0)
        out_ref[m] = (state[...] + (total[0:tok, :] + total[tok:2 * tok, :])).astype(BF16)

        @pl.when(stage < stages - 1)
        def _():
            relay_copy(m, stage + 1).start()

        return carry

    lax.fori_loop(0, micro, one, 0)

    def finish(m, carry):
        for e in range(local):
            arrived(send, m, e, d_send)
            arrived(back, m, e, r_send)

        @pl.when(stage < stages - 1)
        def _():
            relay_copy(m, stage + 1).wait_send()

        return carry

    lax.fori_loop(0, micro, finish, 0)


def solution(mesh):
    stages = mesh.shape["pipe"]
    groups = mesh.shape["exp"] * mesh.shape["pair"]

    def on_device(hidden_in, routes, gate_probs, norm_gain, w_gate, w_up, w_down):
        micro, tok, width = hidden_in.shape
        top = routes.shape[3]
        local, _, units = w_gate.shape[1:]
        experts = local * groups
        cap = max(2, 3 * tok * top // (2 * experts))
        slots = -(-cap // 8) * 8
        span = groups * slots
        vmem = pl.BlockSpec(memory_space=pltpu.VMEM)
        hbm = pl.BlockSpec(memory_space=pl.ANY)
        buffer = pltpu.VMEM((micro, local, groups, slots, width), BF16)
        sem = pltpu.SemaphoreType.DMA((micro, local))
        out = pl.pallas_call(
            functools.partial(kernel, stages, groups, cap),
            out_shape=jax.ShapeDtypeStruct((micro, tok, width), BF16),
            in_specs=[vmem] * 4 + [hbm] * 3,
            out_specs=vmem,
            scratch_shapes=[
                pltpu.VMEM((local, width, units), BF16),
                pltpu.VMEM((local, width, units), BF16),
                pltpu.VMEM((local, units, width), BF16),
                buffer, buffer, buffer, buffer,
                pltpu.VMEM((micro, tok, width), BF16),
                pltpu.VMEM((tok, width), F32),
                pltpu.VMEM((tok, width), BF16),
                pltpu.VMEM((span, width), BF16),
                pltpu.VMEM((span, units), BF16),
                pltpu.VMEM((2 * tok, width), F32),
                pltpu.VMEM((micro, local * span, tok), BF16),
                pltpu.VMEM((micro, 2 * tok, local * span), BF16),
                pltpu.SemaphoreType.DMA((3, local)),
                sem, sem, sem, sem,
                pltpu.SemaphoreType.DMA((micro,)),
                pltpu.SemaphoreType.DMA((micro,)),
            ],
            compiler_params=pltpu.CompilerParams(collective_id=0, has_side_effects=True, vmem_limit_bytes=67043328),
            name="layers",
        )(hidden_in, routes[0], gate_probs[0], norm_gain, w_gate[0], w_up[0], w_down[0])
        return out[None]

    in_specs = (
        P(None, ("exp", "pair"), None),
        P("pipe", None, ("exp", "pair"), None),
        P("pipe", None, ("exp", "pair"), None),
        P("pipe", None),
        P("pipe", ("exp", "pair"), None, None),
        P("pipe", ("exp", "pair"), None, None),
        P("pipe", ("exp", "pair"), None, None),
    )
    out_specs = P("pipe", None, ("exp", "pair"), None)
    return jax.shard_map(on_device, mesh=mesh, in_specs=in_specs, out_specs=out_specs, check_vma=False)
```

time: 813 us -> 263 us (0.32)
  the two profiles are of different devices: /device:TPU:1 before, /device:TPU:17 now
where the time goes in v1:
time: 263 us
  Pallas kernels  258 us (98%)
  local copies, waits for them, and re-layouts  4.73 us (2%)
    pallas_call x1, Pallas kernels, on_device(): pl.pallas_call(functools.partial(kernel, stages, groups, cap), out_shape=...  258 us

profile of v1, /device:TPU:17, one launch (start us, length us, event | category | flops | bytes accessed | tf_op | source)
XLA Modules:
  0.0 262.8 jit_solution(12971454888025606114)
XLA Ops:
  0.0 1.4 copy.8
  1.4 1.4 copy.9
  2.8 258.0 %layers.1 = bf16[4,32,2048]{2,1,0:T(8,128)(2,1)} custom-call(bf16[4,32,2048]{2,1,0:T(8,128)(2,1)} %hidden_ref.1, s32[4,32,8]{2,1,0:T(8,128)} %bitcast.10, f32[4,32,8]{2,1,0:T(8,128)} %bitcast.11, f32[1,2048]{1,0:T(1,128)} %gain_ref.1, bf16[2,2048,768]{2,1,0:T(8,128)(2,1)} %bitcast.6, bf16[2,2048,768]{2,1,0:T(8,128)(2,1)} %bitcast.7, ...), custom_call_target="tpu_custom_call" | custom-call | tf_op jit(solution)/shard_map/layers/pallas_call | solution.py:208
  260.9 1.9 copy.11

commit v2 on v1

v2 whole, which is shorter than its diff:
```python
import functools

import jax
import jax.numpy as jnp
from jax import lax
from jax.experimental import pallas as pl
from jax.experimental.pallas import tpu as pltpu
from jax.sharding import PartitionSpec as P

EPS = 1e-06
MESH = pl.DeviceIdType.MESH
BF16 = jnp.bfloat16
F32 = jnp.float32
SIDE = 4
COLS = 256
PARTS = 2


def kernel(stages, groups, cap, hidden_ref, routes_ref, probs_ref, gain_ref, wg_hbm, wu_hbm, wd_hbm, out_ref,
           wg, wu, wd, send, recv, back, done, relay, state, normed, rows, hid, sums, total, pick, mix,
           w_sem, d_send, d_recv, r_send, r_recv, n_send, n_recv):
    stage, exp, pair = lax.axis_index("pipe"), lax.axis_index("exp"), lax.axis_index("pair")
    pairs = lax.axis_size("pair")
    me = exp * pairs + pair
    micro, tok, width = hidden_ref.shape
    top = routes_ref.shape[1]
    local, _, slots, _ = send.shape[1:]
    span = groups * slots
    hidden_units = wg.shape[2]
    part = width // PARTS

    def weight_copies(e):
        return [pltpu.make_async_copy(hbm.at[e], vmem.at[e], w_sem.at[i, e])
                for i, (hbm, vmem) in enumerate(((wg_hbm, wg), (wu_hbm, wu), (wd_hbm, wd)))]

    for e in range(local):
        for copy in weight_copies(e):
            copy.start()

    barrier = pltpu.get_barrier_semaphore()

    def greet(i, carry):
        peer = lax.rem(me + i, groups)
        pl.semaphore_signal(barrier, inc=1, device_id=(stage, peer // pairs, lax.rem(peer, pairs)), device_id_type=MESH)
        return carry

    lax.fori_loop(1, groups, greet, 0)

    @pl.when(stage > 0)
    def _():
        pl.semaphore_signal(barrier, inc=1, device_id=(stage - 1, exp, pair), device_id_type=MESH)

    def prepare(m):
        column = lax.broadcasted_iota(jnp.int32, (tok, local * groups), 1)
        expert = lax.rem(column, groups) * local + column // groups
        probs = probs_ref[m].T
        probs = probs / jnp.sum(probs, axis=-1, keepdims=True)
        routes = routes_ref[m].T
        named = jnp.zeros((tok, local * groups), F32)
        weight = jnp.zeros((tok, local * groups), F32)
        for k in range(top):
            hit = routes[:, k:k + 1] == expert
            named = named + jnp.where(hit, 1.0, 0.0)
            weight = weight + jnp.where(hit, probs[:, k:k + 1], 0.0)
        earlier = lax.broadcasted_iota(jnp.int32, (tok, tok), 1) < lax.broadcasted_iota(jnp.int32, (tok, tok), 0)
        before = jnp.dot(jnp.where(earlier, 1.0, 0.0).astype(BF16), named.astype(BF16), preferred_element_type=F32)
        high = weight.astype(BF16)
        low = (weight - high.astype(F32)).astype(BF16)
        shape = (local * groups, local * span)
        spread = jnp.where(lax.broadcasted_iota(jnp.int32, shape, 1) // slots == lax.broadcasted_iota(jnp.int32, shape, 0), 1.0, 0.0)
        spread = spread.astype(BF16)
        slot = lax.rem(lax.broadcasted_iota(jnp.int32, (tok, local * span), 1), slots).astype(F32)
        taken = jnp.dot(named.astype(BF16), spread, preferred_element_type=F32)
        place = jnp.dot(before.astype(BF16), spread, preferred_element_type=F32)
        mask = jnp.logical_and(taken > 0.5, jnp.abs(place - slot) < 0.5)
        mix[m, 0:tok, :] = jnp.where(mask, jnp.dot(high, spread, preferred_element_type=F32), 0.0).astype(BF16)
        mix[m, tok:2 * tok, :] = jnp.where(mask, jnp.dot(low, spread, preferred_element_type=F32), 0.0).astype(BF16)
        pick[m] = jnp.where(mask, 1.0, 0.0).T.astype(BF16)

    prepare(0)
    pl.semaphore_wait(barrier, groups - 1 + jnp.minimum(stages - 1 - stage, 1))

    offsets = [(dx, dz, dy) for dx in range(SIDE) for dz in range(SIDE) for dy in range(2)][1:]
    offsets.sort(key=lambda o: -(min(o[0], SIDE - o[0]) + min(o[1], SIDE - o[1]) + o[2]))

    def exchange(source, target, m, e, h, s_sem, r_sem):
        x, z = exp // SIDE, lax.rem(exp, SIDE)
        lanes = pl.ds(h * part, part)
        for dx, dz, dy in offsets:
            peer_exp = lax.rem(x + dx, SIDE) * SIDE + lax.rem(z + dz, SIDE)
            peer_pair = lax.rem(pair + dy, pairs)
            peer = peer_exp * pairs + peer_pair
            pltpu.make_async_remote_copy(
                src_ref=source.at[m, e, peer, pl.ds(0, cap), lanes],
                dst_ref=target.at[m, e, me, pl.ds(0, cap), lanes],
                send_sem=s_sem.at[m, e, h],
                recv_sem=r_sem.at[m, e, h],
                device_id=(stage, peer_exp, peer_pair),
                device_id_type=MESH,
            ).start()
        target[m, e, me, :, lanes] = source[m, e, me, :, lanes]

    def arrived(buffer, m, e, h, sem):
        piece = buffer.at[m, e, pl.ds(0, groups - 1), pl.ds(0, cap), pl.ds(h * part, part)]
        pltpu.make_async_copy(piece, piece, sem.at[m, e, h]).wait()

    def relay_copy(m, h, target_stage):
        lanes = pl.ds(h * part, part)
        return pltpu.make_async_remote_copy(
            src_ref=out_ref.at[m, :, lanes], dst_ref=relay.at[m, :, lanes], send_sem=n_send.at[m, h], recv_sem=n_recv.at[m, h],
            device_id=(target_stage, exp, pair), device_id_type=MESH)

    def begin(m):
        @pl.when(stage == 0)
        def _():
            state[m] = hidden_ref[m].astype(F32)

        @pl.when(stage > 0)
        def _():
            for h in range(PARTS):
                relay_copy(m, h, stage).wait_recv()
            state[m] = relay[m].astype(F32)

        floated = state[m]
        scale = lax.rsqrt(jnp.mean(floated * floated, axis=-1, keepdims=True) + EPS)
        normed[...] = (floated * scale * gain_ref[...]).astype(BF16)

        def dispatch(e, carry):
            first = pl.multiple_of(e * span, span)
            for h in range(PARTS):
                for c in range(h * part, (h + 1) * part, COLS):
                    made = jnp.dot(pick[m, pl.ds(first, span), :], normed[:, c:c + COLS], preferred_element_type=F32)
                    send[m, e, :, :, c:c + COLS] = made.reshape(groups, slots, COLS).astype(BF16)
                exchange(send, recv, m, e, h, d_send, d_recv)
            return carry

        lax.fori_loop(0, local, dispatch, 0)

    def experts(m):
        def ffn(e, carry):
            @pl.when(m == 0)
            def _():
                for copy in weight_copies(e):
                    copy.wait()

            for h in range(PARTS):
                arrived(recv, m, e, h, d_recv)
                low, high = h * part, (h + 1) * part
                rows[...] = recv[m, e, :, :, low:high].reshape(span, part)
                for c in range(0, hidden_units, COLS):
                    gate = jnp.dot(rows[...], wg[e, low:high, c:c + COLS], preferred_element_type=F32)
                    upward = jnp.dot(rows[...], wu[e, low:high, c:c + COLS], preferred_element_type=F32)
                    if h > 0:
                        gate = gate + sums[0, :, c:c + COLS]
                        upward = upward + sums[1, :, c:c + COLS]
                    if h < PARTS - 1:
                        sums[0, :, c:c + COLS] = gate
                        sums[1, :, c:c + COLS] = upward
                    else:
                        hid[:, c:c + COLS] = (jax.nn.silu(gate) * upward).astype(BF16)
            for h in range(PARTS):
                for c in range(h * part, (h + 1) * part, COLS):
                    made = jnp.dot(hid[...], wd[e, :, c:c + COLS], preferred_element_type=F32)
                    back[m, e, :, :, c:c + COLS] = made.reshape(groups, slots, COLS).astype(BF16)
                exchange(back, done, m, e, h, r_send, r_recv)
            return carry

        lax.fori_loop(0, local, ffn, 0)

    def end(m):
        for e in range(local):
            for h in range(PARTS):
                arrived(done, m, e, h, r_recv)
                for c in range(h * part, (h + 1) * part, COLS):
                    mixed = jnp.dot(mix[m, :, e * span:(e + 1) * span],
                                    done[m, e, :, :, c:c + COLS].reshape(span, COLS), preferred_element_type=F32)
                    mixed = mixed[0:tok] + mixed[tok:2 * tok]
                    if e == 0:
                        mixed = mixed + state[m, :, c:c + COLS]
                    else:
                        mixed = mixed + total[:, c:c + COLS]
                    if e < local - 1:
                        total[:, c:c + COLS] = mixed
                    else:
                        out_ref[m, :, c:c + COLS] = mixed.astype(BF16)
                if e == local - 1:
                    @pl.when(stage < stages - 1)
                    def _():
                        relay_copy(m, h, stage + 1).start()

    begin(0)

    def one(m, carry):
        more = m + 1 < micro
        ahead = jnp.logical_or(jnp.logical_and(stage == 0, m == 0), jnp.logical_and(stage >= 2, m == 2))

        @pl.when(more)
        def _():
            prepare(m + 1)

        done[m, :, :, cap:slots, :] = jnp.zeros((local, groups, slots - cap, width), BF16)
        experts(m)

        @pl.when(jnp.logical_and(more, ahead))
        def _():
            begin(m + 1)

        end(m)

        @pl.when(jnp.logical_and(more, jnp.logical_not(ahead)))
        def _():
            begin(m + 1)

        return carry

    lax.fori_loop(0, micro, one, 0)

    def finish(m, carry):
        for h in range(PARTS):
            for e in range(local):
                arrived(send, m, e, h, d_send)
                arrived(back, m, e, h, r_send)

            @pl.when(stage < stages - 1)
            def _():
                relay_copy(m, h, stage + 1).wait_send()

        return carry

    lax.fori_loop(0, micro, finish, 0)


def solution(mesh):
    stages = mesh.shape["pipe"]
    groups = mesh.shape["exp"] * mesh.shape["pair"]

    def on_device(hidden_in, routes, gate_probs, norm_gain, w_gate, w_up, w_down):
        micro, tok, width = hidden_in.shape
        top = routes.shape[3]
        local, _, units = w_gate.shape[1:]
        experts = local * groups
        cap = max(2, 3 * tok * top // (2 * experts))
        slots = -(-cap // 8) * 8
        span = groups * slots
        vmem = pl.BlockSpec(memory_space=pltpu.VMEM)
        hbm = pl.BlockSpec(memory_space=pl.ANY)
        buffer = pltpu.VMEM((micro, local, groups, slots, width), BF16)
        sem = pltpu.SemaphoreType.DMA((micro, local, PARTS))
        out = pl.pallas_call(
            functools.partial(kernel, stages, groups, cap),
            out_shape=jax.ShapeDtypeStruct((micro, tok, width), BF16),
            in_specs=[vmem] * 4 + [hbm] * 3,
            out_specs=vmem,
            scratch_shapes=[
                pltpu.VMEM((local, width, units), BF16),
                pltpu.VMEM((local, width, units), BF16),
                pltpu.VMEM((local, units, width), BF16),
                buffer, buffer, buffer, buffer,
                pltpu.VMEM((micro, tok, width), BF16),
                pltpu.VMEM((micro, tok, width), F32),
                pltpu.VMEM((tok, width), BF16),
                pltpu.VMEM((span, width // PARTS), BF16),
                pltpu.VMEM((span, units), BF16),
                pltpu.VMEM((2, span, units), F32),
                pltpu.VMEM((tok, width), F32),
                pltpu.VMEM((micro, local * span, tok), BF16),
                pltpu.VMEM((micro, 2 * tok, local * span), BF16),
                pltpu.SemaphoreType.DMA((3, local)),
                sem, sem, sem, sem,
                pltpu.SemaphoreType.DMA((micro, PARTS)),
                pltpu.SemaphoreType.DMA((micro, PARTS)),
            ],
            compiler_params=pltpu.CompilerParams(collective_id=0, has_side_effects=True, vmem_limit_bytes=67043328),
            name="layers",
        )(hidden_in, jnp.swapaxes(routes[0], 1, 2), jnp.swapaxes(gate_probs[0], 1, 2), norm_gain, w_gate[0], w_up[0], w_down[0])
        return out[None]

    in_specs = (
        P(None, ("exp", "pair"), None),
        P("pipe", None, ("exp", "pair"), None),
        P("pipe", None, ("exp", "pair"), None),
        P("pipe", None),
        P("pipe", ("exp", "pair"), None, None),
        P("pipe", ("exp", "pair"), None, None),
        P("pipe", ("exp", "pair"), None, None),
    )
    out_specs = P("pipe", None, ("exp", "pair"), None)
    return jax.shard_map(on_device, mesh=mesh, in_specs=in_specs, out_specs=out_specs, check_vma=False)
```

time: 263 us -> 237 us (0.901)
  Pallas kernels: 258 us -> 235 us
  local copies, waits for them, and re-layouts: 4.73 us -> 1.88 us
    pallas_call x1, Pallas kernels: 258 us -> 235 us  [on_device(): pl.pallas_call(functools.partial(kernel, stages, groups, cap), out_shape=...]
    unnamed x3 -> x1, local copies, waits for them, and re-layouts: 4.73 us -> 1.88 us
where the time goes in v2:
time: 237 us
  Pallas kernels  235 us (99%)
    pallas_call x1, Pallas kernels, on_device(): pl.pallas_call(functools.partial(kernel, stages, groups, cap), out_shape=...  235 us

profile of v2, /device:TPU:17, one launch (start us, length us, event | category | flops | bytes accessed | tf_op | source)
XLA Modules:
  0.0 237.2 jit_solution(2965548101745950880)
XLA Ops:
  0.0 235.3 %layers.1 = bf16[4,32,2048]{2,1,0:T(8,128)(2,1)} custom-call(bf16[4,32,2048]{2,1,0:T(8,128)(2,1)} %hidden_ref.1, s32[4,8,32]{2,1,0:T(8,128)} %bitcast.14, f32[4,8,32]{2,1,0:T(8,128)} %bitcast.15, f32[1,2048]{1,0:T(1,128)} %gain_ref.1, bf16[2,2048,768]{2,1,0:T(8,128)(2,1)} %bitcast.10, bf16[2,2048,768]{2,1,0:T(8,128)(2,1)} %bitcast.11, ...), custom_call_target="tpu_custom_call" | custom-call | tf_op jit(solution)/shard_map/layers/pallas_call | solution.py:249
  235.3 1.9 copy.9

commit v3 on v2

--- a/solution.py
+++ b/solution.py
@@ -13,7 +13,7 @@
 F32 = jnp.float32
 SIDE = 4
 COLS = 256
-PARTS = 2
+PARTS = 4
 
 
 def kernel(stages, groups, cap, hidden_ref, routes_ref, probs_ref, gain_ref, wg_hbm, wu_hbm, wd_hbm, out_ref,
@@ -192,7 +192,7 @@
 
     def one(m, carry):
         more = m + 1 < micro
-        ahead = jnp.logical_or(jnp.logical_and(stage == 0, m == 0), jnp.logical_and(stage >= 2, m == 2))
+        ahead = ((2304 >> (stage * 3 + m)) & 1) == 1
 
         @pl.when(more)
         def _():

time: 237 us -> 228 us (0.962)
  Pallas kernels: 235 us -> 226 us
    pallas_call x1, Pallas kernels: 235 us -> 226 us  [on_device(): pl.pallas_call(functools.partial(kernel, stages, groups, cap), out_shape=...]
where the time goes in v3:
time: 228 us
  Pallas kernels  226 us (99%)
    pallas_call x1, Pallas kernels, on_device(): pl.pallas_call(functools.partial(kernel, stages, groups, cap), out_shape=...  226 us

profile of v3, /device:TPU:17, one launch (start us, length us, event | category | flops | bytes accessed | tf_op | source)
XLA Modules:
  0.0 228.1 jit_solution(14745189917367094278)
XLA Ops:
  0.0 226.2 %layers.1 = bf16[4,32,2048]{2,1,0:T(8,128)(2,1)} custom-call(bf16[4,32,2048]{2,1,0:T(8,128)(2,1)} %hidden_ref.1, s32[4,8,32]{2,1,0:T(8,128)} %bitcast.14, f32[4,8,32]{2,1,0:T(8,128)} %bitcast.15, f32[1,2048]{1,0:T(1,128)} %gain_ref.1, bf16[2,2048,768]{2,1,0:T(8,128)(2,1)} %bitcast.10, bf16[2,2048,768]{2,1,0:T(8,128)(2,1)} %bitcast.11, ...), custom_call_target="tpu_custom_call" | custom-call | tf_op jit(solution)/shard_map/layers/pallas_call | solution.py:249
  226.2 1.9 copy.9
